TPU v7x, 32 devices: a whole 2x2x4 slice. The times are simulated.
32 devices in a mesh: site: 16 (over z, x, core), sec: 2 (over y).
Axes of the slice: x: 2, y: 2, z: 4, core: 2. Of those that a mesh axis runs over, the one named last changes fastest.
Arguments:
- left_canon: bfloat16 [16, 4, 4, 128, 128], P('site', None, 'sec'), may hold values from -1.5 to 1.5
- right_canon: bfloat16 [16, 4, 4, 128, 128], P('site', None, 'sec'), may hold values from -1.5 to 1.5
- center_site: bfloat16 [16, 4, 4, 128, 128], P('site', None, 'sec'), may hold values from -6 to 6
- center_bond: bfloat16 [16, 4, 128, 128], P('site', 'sec'), may hold values from -2 to 3
- left_seed: bfloat16 [16, 4, 128, 128], P('site', 'sec'), may hold values from -2 to 4
- right_seed: bfloat16 [16, 4, 128, 128], P('site', 'sec'), may hold values from -2 to 4
- left_sector: int32 [16, 4, 4], P('site'), may hold values from 0 to 3, each once within a row
- onsite: float32 [16, 4], P('site'), may hold values from 0.5 to 2
- bond_shift: float32 [16], P('site'), may hold values from 0.5 to 2
Outputs:
- left_new: bfloat16 [16, 4, 4, 128, 128], P('site', None, 'sec')
- right_new: bfloat16 [16, 4, 4, 128, 128], P('site', None, 'sec')
Inputs may be any that keep to these rules, and one draw needn't show every extreme that they name: `left_sector`: for each site and local state the 4 entries are a permutation of the sectors.
All inputs are finite; a program needn't handle non-finite values.
Results may differ from a plain program's by a relative error of at most 0.028.
Values may be sent and summed in bfloat16 or wider, within the bound.
A program may use at most 64 MiB of HBM per device.

v0:
```python
import functools

import jax
import jax.numpy as jnp
from jax import lax
from jax.experimental import pallas as pl
from jax.experimental.pallas import tpu as pltpu
from jax.sharding import PartitionSpec as P

NSI = 10
NAPP = 2
MESH = pl.DeviceIdType.MESH
F32 = jnp.float32
BF16 = jnp.bfloat16


def dot(a, b):
    return lax.dot_general(a, b, (((1,), (0,)), ((), ())), preferred_element_type=F32)


def dot_nt(a, b):
    return lax.dot_general(a, b, (((1,), (1,)), ((), ())), preferred_element_type=F32)


def dot_tn(a, b):
    return lax.dot_general(a, b, (((0,), (0,)), ((), ())), preferred_element_type=F32)


def split(x):
    hi = x.astype(BF16)
    return hi, (x - hi.astype(F32)).astype(BF16)


def as_lhs(pair):
    return jnp.concatenate(pair, axis=1)


def as_rhs(pair):
    row = jnp.concatenate(pair, axis=1)
    return jnp.concatenate((row, row), axis=0)


def mm(lhs_pair, rhs_pair):
    out = dot(as_lhs(lhs_pair), as_rhs(rhs_pair))
    width = out.shape[1] // 2
    return out[:, :width] + out[:, width:]


def kernel(
    steps, sites, parts, phys, owned,
    lc, rc, cs, cb, lseed, rseed, src, onsite, shift,
    left_new, right_new,
    hold_l, lrecv, lsend, rrecv, psend, terms, lct, site, bond, ys, zs, env_r, env_n,
    gsend, grecv, usend, urecv, fsend, frecv, fall, tns, tnr, trs, trr,
    s_ls, s_lr, s_ps, s_pr, s_gs, s_gr, s_us, s_ur, s_fs, s_fr, s_tns, s_tnr, s_trs, s_trr,
):
    j = lax.axis_index("site")
    me = lax.axis_index("sec")
    after, before = lax.rem(j + 1, sites), lax.rem(j + sites - 1, sites)
    off = me * owned
    width = lc.shape[-1]
    sectors = parts * owned

    def sec(d):
        return lax.rem(me + d, parts)

    def copy(a, b, ss, rs, to_site, to_sec):
        return pltpu.make_async_remote_copy(
            src_ref=a, dst_ref=b, send_sem=ss, recv_sem=rs,
            device_id={"site": to_site, "sec": to_sec}, device_id_type=MESH,
        )

    def c_seed(d):
        return copy(lseed.at[0], lrecv.at[0, me], s_ls.at[steps, d], s_lr.at[0, me], j, sec(d))

    def c_left(t, d):
        return copy(lsend.at[t], lrecv.at[t + 1, me], s_ls.at[t, d], s_lr.at[t + 1, me], after, sec(d))

    def c_right(t, d):
        return copy(psend.at[t, d], rrecv.at[t, me], s_ps.at[t, d], s_pr.at[t, me], before, sec(d))

    def c_tn(d):
        return copy(tns, tnr.at[me], s_tns.at[d], s_tnr.at[me], j, sec(d))

    def c_tr(d):
        return copy(trs, trr.at[me], s_trs.at[d], s_trr.at[me], before, sec(d))

    def c_gram(d):
        return copy(gsend.at[d], grecv.at[me], s_gs.at[d], s_gr.at[me], j, sec(d))

    def c_unit():
        return copy(usend, urecv, s_us.at[0], s_ur.at[0], after, me)

    def c_factor(d):
        return copy(fsend, frecv.at[me], s_fs.at[d], s_fr.at[me], j, sec(d))

    def got(ref, sem):
        copy(ref, ref, s_us.at[0], sem, after, me).wait_recv()

    barrier = pltpu.get_barrier_semaphore()
    for d in range(parts):
        for where in (after, before) if d == 0 else (after, before, j):
            pl.semaphore_signal(
                barrier, inc=1, device_id={"site": where, "sec": sec(d)}, device_id_type=MESH
            )
    pl.semaphore_wait(barrier, 3 * parts - 1)

    for d in range(1, parts):
        c_seed(d).start()

    sources = [[src[0, s, off + k] for k in range(owned)] for s in range(phys)]

    def gathered(target, i):
        want = target * owned + i
        total = None
        for s in range(phys):
            hit, at = jnp.int32(0), jnp.int32(0)
            for k in range(owned):
                same = (sources[s][k] == want).astype(jnp.int32)
                hit, at = hit + same, at + same * k
            term = terms[s * owned + at] * hit.astype(F32)
            total = term if total is None else total + term
        return total

    for k in range(owned):
        for s in range(phys):
            lct[k, :, s * width : (s + 1) * width] = lc[0, s, k].T
    for k in range(owned):
        env_r[k] = rseed[0, k]
        hold_l[off + k] = lseed[0, k]
    def seed_arrival():
        for d in range(1, parts):
            a = sec(d)
            got(lrecv.at[0, a], s_lr.at[0, a])
            for k in range(owned):
                hold_l[a * owned + k] = lrecv[0, a, k]

    def left_arrival(t):
        for d in range(parts):
            a = sec(d)
            got(lrecv.at[t, a], s_lr.at[t, a])
            for k in range(owned):
                hold_l[a * owned + k] = lrecv[t, a, k]

    def right_arrival(t):
        for d in range(parts):
            a = sec(d)
            got(rrecv.at[t, a], s_pr.at[t, a])
        for k in range(owned):
            total = rrecv[t, 0, k].astype(F32)
            for a in range(1, parts):
                total = total + rrecv[t, a, k].astype(F32)
            env_r[k] = total.astype(BF16)

    def turn(t, carry):
        @pl.when(t > 0)
        def _():
            right_arrival(t - 1)

        for k in range(owned):
            stack = jnp.concatenate([rc[0, s, k] for s in range(phys)], axis=0)
            prod = dot(stack, env_r[k]).astype(BF16)
            for s in range(phys):
                terms[s * owned + k] = dot_nt(prod[s * width : (s + 1) * width], rc[0, s, k])
        for d in range(parts):
            for i in range(owned):
                psend[t, d, i] = gathered(sec(d), i).astype(BF16)
            c_right(t, d).start()

        @pl.when(t == 0)
        def _():
            seed_arrival()

        @pl.when(t > 0)
        def _():
            left_arrival(t)

        for k in range(owned):
            prods = [
                dot(hold_l[sources[s][k]], lc[0, s, k]).astype(BF16) for s in range(phys)
            ]
            lsend[t, k] = dot(lct[k], jnp.concatenate(prods, axis=0)).astype(BF16)
        for d in range(parts):
            c_left(t, d).start()

        return carry

    lax.fori_loop(0, steps, turn, 0)

    rows = lax.broadcasted_iota(jnp.int32, (width, width), 0)
    cols = lax.broadcasted_iota(jnp.int32, (width, width), 1)
    diagonal = (rows == cols).astype(F32)

    def traces(blocks):
        total = None
        for block in blocks:
            total = block.astype(F32) if total is None else total + block.astype(F32)
        return jnp.sum((total * diagonal).reshape(width // 8, 8, width), axis=0)

    tns[...] = traces([lsend[steps - 1, k] for k in range(owned)])
    for d in range(1, parts):
        c_tn(d).start()
    trs[...] = traces([psend[steps - 1, d, i] for d in range(parts) for i in range(owned)])
    for d in range(parts):
        c_tr(d).start()

    def scale_of(total):
        return (sectors * width) / jnp.sum(total, axis=(0, 1), keepdims=True)

    total = tns[...]
    for d in range(1, parts):
        a = sec(d)
        got(tnr.at[a], s_tnr.at[a])
        total = total + tnr[a]
    scale = scale_of(total)
    for k in range(owned):
        env_n[k] = (lsend[steps - 1, k].astype(F32) * scale).astype(BF16)

    left_arrival(steps)
    scale = scale_of(traces([hold_l[m] for m in range(sectors)]))
    for m in range(sectors):
        hold_l[m] = (hold_l[m].astype(F32) * scale).astype(BF16)

    right_arrival(steps - 1)
    for a in range(parts):
        got(trr.at[a], s_trr.at[a])
    total = trr[0]
    for a in range(1, parts):
        total = total + trr[a]
    scale = scale_of(total)
    for k in range(owned):
        env_r[k] = (env_r[k].astype(F32) * scale).astype(BF16)

    for k in range(owned):
        for s in range(phys):
            site[k, s * width : (s + 1) * width] = cs[0, s, k]
        bond[k] = cb[0, k]
    for repeat in range(NAPP):
        for k in range(owned):
            halves = [
                dot(hold_l[sources[s][k]], site[k, s * width : (s + 1) * width]).astype(BF16)
                for s in range(phys)
            ]
            whole = dot(jnp.concatenate(halves, axis=0), env_r[k])
            for s in range(phys):
                part = slice(s * width, (s + 1) * width)
                site[k, part] = (whole[part] + onsite[0, s] * site[k, part].astype(F32)).astype(BF16)

    for k in range(owned):
        for s in range(phys):
            block = site[k, s * width : (s + 1) * width]
            terms[s * owned + k] = dot_nt(block, block)
    for d in range(parts - 1, -1, -1):
        for i in range(owned):
            gsend[d, i] = gathered(sec(d), i)
        if d > 0:
            c_gram(d).start()

    for repeat in range(NAPP):
        for k in range(owned):
            half = dot(env_n[k], bond[k]).astype(BF16)
            bond[k] = (dot(half, env_r[k]) + shift[0] * bond[k].astype(F32)).astype(BF16)

    def inverse_roots(grams):
        norms = []
        for i, gram in enumerate(grams):
            norm = jnp.sqrt(jnp.sum(gram * gram, axis=(0, 1), keepdims=True))
            norms.append(norm)
            upper = gram / norm
            middle = 1.5 * diagonal - 0.5 * upper
            ys[i] = mm(split(upper), split(middle))
            zs[i] = middle

        def body(n, carry):
            uppers = [split(ys[i]) for i in range(len(grams))]
            lowers = [split(zs[i]) for i in range(len(grams))]
            middles = [
                split(1.5 * diagonal - 0.5 * mm(z, y)) for z, y in zip(lowers, uppers)
            ]
            for i in range(len(grams)):
                ys[i] = mm(uppers[i], middles[i])
                zs[i] = mm(middles[i], lowers[i])
            return carry

        lax.fori_loop(0, NSI - 2, body, 0)
        for i in range(len(grams)):
            lower = split(zs[i])
            middle = split(1.5 * diagonal - 0.5 * mm(lower, split(ys[i])))
            zs[i] = mm(middle, lower) / jnp.sqrt(norms[i])

    inverse_roots(
        [dot_tn(bond[k], bond[k]) for k in range(owned)]
        + [dot_tn(site[k], site[k]) for k in range(owned)]
    )
    factors = []
    for k in range(owned):
        hi, lo = split(zs[k])
        unit_t = dot_nt(hi, bond[k]) + dot_nt(lo, bond[k])
        usend[k] = unit_t.astype(BF16)
        factors.append(mm(split(zs[owned + k]), split(unit_t)).astype(BF16))
    c_unit().start()

    for d in range(1, parts):
        a = sec(d)
        got(grecv.at[a], s_gr.at[a])
    grams = []
    for i in range(owned):
        total = gsend[0, i]
        for d in range(1, parts):
            total = total + grecv[sec(d), i]
        grams.append(total)
    inverse_roots(grams)
    got(urecv, s_ur.at[0])
    for i in range(owned):
        hi, lo = split(zs[i])
        fsend[i] = (dot(urecv[i], hi) + dot(urecv[i], lo)).astype(BF16)
    for d in range(1, parts):
        c_factor(d).start()

    for k in range(owned):
        whole = dot(site[k], factors[k]).astype(BF16)
        for s in range(phys):
            left_new[0, s, k] = whole[s * width : (s + 1) * width]
    for i in range(owned):
        fall[off + i] = fsend[i]
    for d in range(1, parts):
        a = sec(d)
        got(frecv.at[a], s_fr.at[a])
        for i in range(owned):
            fall[a * owned + i] = frecv[a, i]
    for k in range(owned):
        for s in range(phys):
            block = site[k, s * width : (s + 1) * width]
            right_new[0, s, k] = dot(fall[sources[s][k]], block).astype(BF16)

    def drain(t, carry):
        for d in range(parts):
            c_left(t, d).wait_send()
            c_right(t, d).wait_send()
        return carry

    lax.fori_loop(0, steps, drain, 0)
    for d in range(parts):
        c_tr(d).wait_send()
    for d in range(1, parts):
        for c in (c_seed, c_tn, c_gram, c_factor):
            c(d).wait_send()
    c_unit().wait_send()


def per_device(lc, rc, cs, cb, lseed, rseed, src, onsite, shift):
    sites, parts = lax.axis_size("site"), lax.axis_size("sec")
    steps = sites // 4
    _, phys, owned, width, _ = lc.shape
    sectors = parts * owned
    block = (width, width)
    most = 2 * owned

    def vm(*shape, dtype=BF16):
        return pltpu.VMEM(shape, dtype)

    def dma(*shape):
        return pltpu.SemaphoreType.DMA(shape)

    in_vmem = pl.BlockSpec(memory_space=pltpu.VMEM)
    in_smem = pl.BlockSpec(memory_space=pltpu.SMEM)
    shape = jax.ShapeDtypeStruct(cs.shape, BF16)
    return pl.pallas_call(
        functools.partial(kernel, steps, sites, parts, phys, owned),
        out_shape=(shape, shape),
        in_specs=[in_vmem] * 6 + [in_smem] * 3,
        out_specs=(in_vmem, in_vmem),
        scratch_shapes=[
            vm(sectors, *block),
            vm(steps + 1, parts, owned, *block),
            vm(steps, owned, *block),
            vm(steps, parts, owned, *block),
            vm(steps, parts, owned, *block),
            vm(phys * owned, *block, dtype=F32),
            vm(owned, width, phys * width),
            vm(owned, phys * width, width),
            vm(owned, *block),
            vm(most, *block, dtype=F32),
            vm(most, *block, dtype=F32),
            vm(owned, *block),
            vm(owned, *block),
            vm(parts, owned, *block, dtype=F32),
            vm(parts, owned, *block, dtype=F32),
            vm(owned, *block),
            vm(owned, *block),
            vm(owned, *block),
            vm(parts, owned, *block),
            vm(sectors, *block),
            vm(8, width, dtype=F32),
            vm(parts, 8, width, dtype=F32),
            vm(8, width, dtype=F32),
            vm(parts, 8, width, dtype=F32),
            dma(steps + 1, parts), dma(steps + 1, parts),
            dma(steps, parts), dma(steps, parts),
            dma(parts), dma(parts),
            dma(1), dma(1),
            dma(parts), dma(parts),
            dma(parts), dma(parts),
            dma(parts), dma(parts),
        ],
        compiler_params=pltpu.CompilerParams(
            collective_id=0, has_side_effects=True, vmem_limit_bytes=60 * 1024 * 1024
        ),
    )(lc, rc, cs, cb, lseed, rseed, src, onsite, shift)


def solution(mesh):
    tensor = P("site", None, "sec", None, None)
    blocks = P("site", "sec", None, None)
    return jax.shard_map(
        per_device,
        mesh=mesh,
        in_specs=(tensor, tensor, tensor, blocks, blocks, blocks,
                  P("site", None, None), P("site", None), P("site")),
        out_specs=(tensor, tensor),
        check_vma=False,
    )
```

profile of v0, /device:TPU:0, one launch (start us, length us, event | category | flops | bytes accessed | tf_op | source)
XLA Modules:
  0.0 49.5 jit_solution(5098223935879853678)
XLA Ops:
  1.3 45.8 %shard_map.104 = (bf16[1,4,2,128,128]{4,3,2,1,0:T(8,128)(2,1)}, bf16[1,4,2,128,128]{4,3,2,1,0:T(8,128)(2,1)}) custom-call(bf16[1,4,2,128,128]{4,3,2,1,0:T(8,128)(2,1)} %lc.1, bf16[1,4,2,128,128]{4,3,2,1,0:T(8,128)(2,1)} %rc.1, bf16[1,4,2,128,128]{4,3,2,1,0:T(8,128)(2,1)} %cs.1, bf16[1,2,128,128]{3,2,1,0:T(8,128)(2,1)} %cb.1, bf16[1,2,128,128]{3,2,1,0:T(8,128)(2,1)} %lseed.1, ...), custom_call_target="tpu_custom_call" | custom-call | tf_op jit(solution)/shard_map/pallas_call | solution.py:368
  47.1 0.0 copy-start
  47.1 1.7 %copy.14 = bf16[1,4,2,128,128]{4,3,2,1,0:T(8,128)(2,1)} copy(bf16[1,4,2,128,128]{4,3,2,1,0:T(8,128)(2,1)} %get-tuple-element.4) | data formatting | bytes 524288
  48.8 0.0 copy-done
  48.8 0.7 %copy.15 = bf16[1,4,2,128,128]{4,3,2,1,0:T(8,128)(2,1)} copy(bf16[1,4,2,128,128]{4,3,2,1,0:T(8,128)(2,1)S(1)} %copy-done) | data formatting | bytes 524288
Async XLA Ops:
  47.1 1.7 %copy-start = (bf16[1,4,2,128,128]{4,3,2,1,0:T(8,128)(2,1)S(1)}, bf16[1,4,2,128,128]{4,3,2,1,0:T(8,128)(2,1)}, u32[]{:S(2)}) copy-start(bf16[1,4,2,128,128]{4,3,2,1,0:T(8,128)(2,1)} %get-tuple-element.5) | copy-start | bytes 786436
where the time goes:
time: 49.7 us; the launch traced here: 49.5 us
  Pallas kernels  45.8 us (92%)
  local copies, waits for them, and re-layouts  2.42 us (5%)
  between operations  1.3 us (3%)
    pallas_call x1, Pallas kernels, per_device(): pl.pallas_call(functools.partial(kernel, steps, sites, parts, phys, owned...  45.8 us
    unnamed x4, local copies, waits for them, and re-layouts  2.42 us

commit v1 on v0

v1 whole, which is shorter than its diff:
```python
import functools

import jax
import jax.numpy as jnp
from jax import lax
from jax.experimental import pallas as pl
from jax.experimental.pallas import tpu as pltpu
from jax.sharding import PartitionSpec as P

NSI = 10
NAPP = 2
EARLY = 3
VMEM_BYTES = 67043328
RESERVED = 10240 * 1024
SLACK = 44 * 1024
MESH = pl.DeviceIdType.MESH
F32 = jnp.float32
BF16 = jnp.bfloat16


def dot(a, b):
    return lax.dot_general(a, b, (((1,), (0,)), ((), ())), preferred_element_type=F32)


def dot_nt(a, b):
    return lax.dot_general(a, b, (((1,), (1,)), ((), ())), preferred_element_type=F32)


def dot_tn(a, b):
    return lax.dot_general(a, b, (((0,), (0,)), ((), ())), preferred_element_type=F32)


def split(x):
    hi = x.astype(BF16)
    return hi, (x - hi.astype(F32)).astype(BF16)


def beside(pair):
    return jnp.concatenate(pair, axis=1)


def below(pair):
    return jnp.concatenate(pair, axis=0)


def twice_wide(x):
    return beside((x, x))


def twice_tall(x):
    return below((x, x))


def kernel(
    steps, sites, parts, phys, owned,
    lc_in, rc_in, cs_in, cb_in, lseed_in, rseed_in, src, onsite, shift,
    *refs,
):
    blocks = phys * owned
    left_new, right_new = refs[:blocks], refs[blocks : 2 * blocks]
    (
    lc, rc, cs, cb, lseed, rseed, site, fall,
    hold_l, lrecv, lsend, rrecv, psend, terms, lct, bond, ys, zs, env_r,
    gsend, grecv, usend, urecv, tns, tnr, trs, trr,
    s_in, s_ls, s_lr, s_ps, s_pr, s_gs, s_gr, s_us, s_ur, s_tns, s_tnr, s_trs, s_trr,
    ) = refs[2 * blocks :]
    j = lax.axis_index("site")
    me = lax.axis_index("sec")
    after, before = lax.rem(j + 1, sites), lax.rem(j + sites - 1, sites)
    off = me * owned
    width = lc.shape[-1]
    sectors = parts * owned
    pairs = sectors // 2

    def load(i, a, b):
        return pltpu.make_async_copy(a, b, s_in.at[i])

    loads = [
        load(0, lseed_in, lseed), load(1, rseed_in, rseed), load(2, rc_in, rc),
        load(3, lc_in, lc), load(4, cb_in, cb), load(5, cs_in, cs),
    ]
    for c in loads:
        c.start()

    def sec(d):
        return lax.rem(me + d, parts)

    def copy(a, b, ss, rs, to_site, to_sec):
        return pltpu.make_async_remote_copy(
            src_ref=a, dst_ref=b, send_sem=ss, recv_sem=rs,
            device_id={"site": to_site, "sec": to_sec}, device_id_type=MESH,
        )

    def c_seed(d):
        return copy(lseed.at[0], lrecv.at[0, me], s_ls.at[steps, d], s_lr.at[0, me], j, sec(d))

    def c_left(t, d):
        return copy(lsend.at[t], lrecv.at[t + 1, me], s_ls.at[t, d], s_lr.at[t + 1, me], after, sec(d))

    def c_right(t, d):
        return copy(psend.at[t, d], rrecv.at[t, me], s_ps.at[t, d], s_pr.at[t, me], before, sec(d))

    def c_tn(d):
        return copy(tns, tnr.at[me], s_tns.at[d], s_tnr.at[me], j, sec(d))

    def c_tr(d):
        return copy(trs, trr.at[me], s_trs.at[d], s_trr.at[me], before, sec(d))

    def c_gram(d, p):
        return copy(gsend.at[p], grecv.at[me, p], s_gs.at[d, p], s_gr.at[me, p], j, sec(d))

    def c_unit(d):
        return copy(usend, urecv.at[me], s_us.at[d], s_ur.at[me], after, sec(d))

    def got(ref, sem):
        copy(ref, ref, s_us.at[0], sem, after, me).wait_recv()

    barrier = pltpu.get_barrier_semaphore()
    for d in range(parts):
        for where in (after, before) if d == 0 else (after, before, j):
            pl.semaphore_signal(
                barrier, inc=1, device_id={"site": where, "sec": sec(d)}, device_id_type=MESH
            )
    loads[0].wait()
    pl.semaphore_wait(barrier, 3 * parts - 1)
    for d in range(1, parts):
        c_seed(d).start()

    sources = [[src[0, s, off + k] for k in range(owned)] for s in range(phys)]

    def gathered(target):
        total = None
        for s in range(phys):
            hit, at = jnp.int32(0), jnp.int32(0)
            for k in range(owned):
                same = (sources[s][k] == target).astype(jnp.int32)
                hit, at = hit + same, at + same * k
            term = terms[s * owned + at] * hit.astype(F32)
            total = term if total is None else total + term
        return total

    rows = lax.broadcasted_iota(jnp.int32, (width, width), 0)
    cols = lax.broadcasted_iota(jnp.int32, (width, width), 1)
    diagonal = (rows == cols).astype(F32)
    half_diagonal = 0.5 * diagonal

    def traces(blocks):
        total = None
        for block in blocks:
            total = block.astype(F32) if total is None else total + block.astype(F32)
        return jnp.sum((total * diagonal).reshape(width // 8, 8, width), axis=0)

    loads[1].wait()
    for k in range(owned):
        env_r[k] = rseed[0, k]
    loads[2].wait()

    def seed_arrival():
        for k in range(owned):
            hold_l[off + k] = lseed[0, k]
        for d in range(1, parts):
            a = sec(d)
            got(lrecv.at[0, a], s_lr.at[0, a])
            for k in range(owned):
                hold_l[a * owned + k] = lrecv[0, a, k]

    def left_arrival(t):
        for d in range(parts):
            a = sec(d)
            got(lrecv.at[t, a], s_lr.at[t, a])
            for k in range(owned):
                hold_l[a * owned + k] = lrecv[t, a, k]

    def right_arrival(t):
        for d in range(parts):
            a = sec(d)
            got(rrecv.at[t, a], s_pr.at[t, a])
        for k in range(owned):
            total = rrecv[t, 0, k].astype(F32)
            for a in range(1, parts):
                total = total + rrecv[t, a, k].astype(F32)
            env_r[k] = total.astype(BF16)

    def right_compute(t, last):
        for k in range(owned):
            stack = jnp.concatenate([rc[0, s, k] for s in range(phys)], axis=0)
            prod = dot(stack, env_r[k]).astype(BF16)
            for s in range(phys):
                terms[s * owned + k] = dot_nt(prod[s * width : (s + 1) * width], rc[0, s, k])
        for d in range(parts - 1, -1, -1):
            for i in range(owned):
                psend[t, d, i] = gathered(sec(d) * owned + i).astype(BF16)
            if not last:
                c_right(t, d).start()
        if last:
            trs[...] = traces([psend[t, d, i] for d in range(parts) for i in range(owned)])
            for d in range(parts - 1, -1, -1):
                c_tr(d).start()
            for d in range(parts - 1, -1, -1):
                c_right(t, d).start()

    def left_compute(t, last):
        for k in range(owned):
            prods = [
                dot(hold_l[sources[s][k]], lc[0, s, k]).astype(BF16) for s in range(phys)
            ]
            lsend[t, k] = dot(lct[k], jnp.concatenate(prods, axis=0)).astype(BF16)
        if last:
            tns[...] = traces([lsend[t, k] for k in range(owned)])
            for d in range(1, parts):
                c_tn(d).start()
        for d in range(parts - 1, -1, -1):
            c_left(t, d).start()

    right_compute(0, steps == 1)
    loads[3].wait()
    for k in range(owned):
        for s in range(phys):
            lct[k, :, s * width : (s + 1) * width] = lc[0, s, k].T
    seed_arrival()
    left_compute(0, steps == 1)

    def turn(t, carry):
        right_arrival(t - 1)
        right_compute(t, False)
        left_arrival(t)
        left_compute(t, False)
        return carry

    lax.fori_loop(1, steps - 1, turn, 0)
    if steps > 1:
        right_arrival(steps - 2)
        right_compute(steps - 1, True)
        left_arrival(steps - 1)
        left_compute(steps - 1, True)

    def scale_of(total):
        return (sectors * width) / jnp.sum(total, axis=(0, 1), keepdims=True)

    def begin(i, y, z, gram):
        norm = jnp.sqrt(jnp.sum(gram * gram, axis=(0, 1), keepdims=True))
        root = lax.rsqrt(norm)
        delta = (half_diagonal - 0.5 * (gram / norm)).astype(BF16)
        if z is None:
            y = gram / norm
            zs[i] = diagonal + delta.astype(F32)
        else:
            y, z = y * root, z * root
            zs[i] = z + dot(twice_wide(delta), below(split(z)))
        ys[i] = y + dot(beside(split(y)), twice_tall(delta))
        return root

    def deltas(these):
        zh = [split(zs[i]) for i in these]
        yh = [split(ys[i]) for i in these]
        found = [
            (half_diagonal - 0.5 * dot(z[0], y[0])).astype(BF16) for z, y in zip(zh, yh)
        ]
        return zh, yh, found

    def advance(these):
        zh, yh, found = deltas(these)
        for i, z, y, delta in zip(these, zh, yh, found):
            ys[i] = ys[i] + dot(beside(y), twice_tall(delta))
            zs[i] = zs[i] + dot(twice_wide(delta), below(z))

    def loop(count, these):
        def body(n, carry):
            advance(these)
            return carry

        lax.fori_loop(0, count, body, 0)

    bonds = list(range(owned))
    lefts = [owned + k for k in range(owned)]
    rights = [2 * owned + m for m in range(sectors)]

    right_arrival(steps - 1)
    for a in range(parts):
        got(trr.at[a], s_trr.at[a])
    total = trr[0]
    for a in range(1, parts):
        total = total + trr[a]
    scale = scale_of(total)
    for k in range(owned):
        env_r[k] = (env_r[k].astype(F32) * scale).astype(BF16)

    total = tns[...]
    for d in range(1, parts):
        a = sec(d)
        got(tnr.at[a], s_tnr.at[a])
        total = total + tnr[a]
    scale = scale_of(total)
    loads[4].wait()
    now = [cb[0, k] for k in range(owned)]
    for repeat in range(NAPP):
        for k in range(owned):
            half = dot(lsend[steps - 1, k], now[k]).astype(BF16)
            now[k] = (dot(half, env_r[k]) * scale + shift[0] * now[k].astype(F32)).astype(BF16)
    for k in range(owned):
        begin(k, now[k].astype(F32), now[k].astype(F32).T, dot_tn(now[k], now[k]))
    loads[5].wait()
    for k in range(owned):
        for s in range(phys):
            site[k, s * width : (s + 1) * width] = cs[0, s, k]
    loop(EARLY, bonds)

    left_arrival(steps)
    scale = scale_of(traces([hold_l[m] for m in range(sectors)]))
    for repeat in range(NAPP):
        for k in range(owned):
            halves = [
                dot(hold_l[sources[s][k]], site[k, s * width : (s + 1) * width]).astype(BF16)
                for s in range(phys)
            ]
            whole = dot(jnp.concatenate(halves, axis=0), env_r[k]) * scale
            for s in range(phys):
                part = slice(s * width, (s + 1) * width)
                site[k, part] = (whole[part] + onsite[0, s] * site[k, part].astype(F32)).astype(BF16)

    for k in range(owned):
        for s in range(phys):
            block = site[k, s * width : (s + 1) * width]
            terms[s * owned + k] = dot_nt(block, block)
    for p in range(pairs):
        even, odd = gathered(2 * p), gathered(2 * p + 1)
        gsend[p, :width] = jnp.where(rows >= cols, even, odd)
        gsend[p, width:] = jnp.sum((odd * diagonal).reshape(width // 8, 8, width), axis=0)
        for d in range(1, parts):
            c_gram(d, p).start()

    left_root = [
        begin(lefts[k], None, None, dot_tn(site[k], site[k])) for k in range(owned)
    ]
    loop(NSI - 1 - EARLY, bonds + lefts)
    for k in range(owned):
        usend[k] = zs[k].astype(BF16)
    for d in range(parts - 1, -1, -1):
        c_unit(d).start()
    loop(EARLY - 1, lefts)
    zh, yh, found = deltas(lefts)
    for k in range(owned):
        hi, lo = split(zs[k])
        wide = dot(beside(zh[k]), beside((twice_tall(hi), twice_tall(lo))))
        value = wide[:, :width] + wide[:, width:]
        factor = value + dot(twice_wide(found[k]), below(split(value)))
        whole = dot(site[k], (factor * left_root[k]).astype(BF16)).astype(BF16)
        for s in range(phys):
            left_new[s * owned + k][...] = whole[s * width : (s + 1) * width]

    right_root = []
    for p in range(pairs):
        total, edge = gsend[p, :width], gsend[p, width:]
        for d in range(1, parts):
            a = sec(d)
            got(grecv.at[a, p], s_gr.at[a, p])
            total, edge = total + grecv[a, p, :width], edge + grecv[a, p, width:]
        turned = total.T
        line = jnp.sum(edge, axis=0, keepdims=True)
        right_root.append(begin(rights[2 * p], None, None, jnp.where(rows >= cols, total, turned)))
        odd = jnp.where(rows < cols, total, jnp.where(rows == cols, line, turned))
        right_root.append(begin(rights[2 * p + 1], None, None, odd))
    loop(NSI - 2, rights)
    zh, yh, found = deltas(rights)
    for a in range(parts):
        got(urecv.at[a], s_ur.at[a])
    for m in range(sectors):
        unit = urecv[m // owned, m % owned]
        value = dot(twice_wide(unit), below(zh[m]))
        factor = value + dot(beside(split(value)), twice_tall(found[m]))
        fall[m] = (factor * right_root[m]).astype(BF16)
    for k in range(owned):
        for s in range(phys):
            block = site[k, s * width : (s + 1) * width]
            right_new[s * owned + k][...] = dot(fall[sources[s][k]], block).astype(BF16)

    def drain(t, carry):
        for d in range(parts):
            c_left(t, d).wait_send()
            c_right(t, d).wait_send()
        return carry

    lax.fori_loop(0, steps, drain, 0)
    for d in range(parts):
        c_tr(d).wait_send()
        c_unit(d).wait_send()
    for d in range(1, parts):
        c_seed(d).wait_send()
        c_tn(d).wait_send()
        for p in range(pairs):
            c_gram(d, p).wait_send()


def finish(phys, owned, *refs):
    blocks = phys * owned
    left_new, right_new, sems = refs[2 * blocks :]
    copies = []
    for i in range(2 * blocks):
        out = left_new if i < blocks else right_new
        s, k = (i % blocks) // owned, i % owned
        copies.append(pltpu.make_async_copy(refs[i], out.at[0, s, k], sems.at[i]))
        copies[-1].start()
    for c in copies:
        c.wait()


def per_device(lc, rc, cs, cb, lseed, rseed, src, onsite, shift):
    sites, parts = lax.axis_size("site"), lax.axis_size("sec")
    steps = sites // 4
    _, phys, owned, width, _ = lc.shape
    sectors = parts * owned
    pairs = sectors // 2
    block = (width, width)

    def vm(*shape, dtype=BF16):
        return pltpu.VMEM(shape, dtype)

    def dma(*shape):
        return pltpu.SemaphoreType.DMA(shape)

    in_hbm = pl.BlockSpec(memory_space=pltpu.HBM)
    in_vmem = pl.BlockSpec(memory_space=pltpu.VMEM)
    in_smem = pl.BlockSpec(memory_space=pltpu.SMEM)
    shape = jax.ShapeDtypeStruct(cs.shape, BF16)
    blocks = phys * owned
    room = VMEM_BYTES - RESERVED - 2 * cs.size * 2 - SLACK
    done = pl.pallas_call(
        functools.partial(kernel, steps, sites, parts, phys, owned),
        out_shape=[jax.ShapeDtypeStruct(block, BF16)] * (2 * blocks),
        in_specs=[in_hbm] * 6 + [in_smem] * 3,
        out_specs=[in_vmem] * (2 * blocks),
        scratch_shapes=[
            vm(*lc.shape), vm(*rc.shape), vm(*cs.shape), vm(*cb.shape),
            vm(*lseed.shape), vm(*rseed.shape),
            vm(owned, phys * width, width), vm(sectors, *block),
            vm(sectors, *block),
            vm(steps + 1, parts, owned, *block),
            vm(steps, owned, *block),
            vm(steps, parts, owned, *block),
            vm(steps, parts, owned, *block),
            vm(phys * owned, *block, dtype=F32),
            vm(owned, width, phys * width),
            vm(owned, *block),
            vm(2 * owned + sectors, *block, dtype=F32),
            vm(2 * owned + sectors, *block, dtype=F32),
            vm(owned, *block),
            vm(pairs, width + 8, width, dtype=F32),
            vm(parts, pairs, width + 8, width, dtype=F32),
            vm(owned, *block),
            vm(parts, owned, *block),
            vm(8, width, dtype=F32),
            vm(parts, 8, width, dtype=F32),
            vm(8, width, dtype=F32),
            vm(parts, 8, width, dtype=F32),
            dma(6),
            dma(steps + 1, parts), dma(steps + 1, parts),
            dma(steps, parts), dma(steps, parts),
            dma(parts, pairs), dma(parts, pairs),
            dma(parts), dma(parts),
            dma(parts), dma(parts),
            dma(parts), dma(parts),
        ],
        compiler_params=pltpu.CompilerParams(
            collective_id=0, has_side_effects=True, vmem_limit_bytes=room
        ),
    )(lc, rc, cs, cb, lseed, rseed, src, onsite, shift)
    return pl.pallas_call(
        functools.partial(finish, phys, owned),
        out_shape=(shape, shape),
        in_specs=[in_vmem] * (2 * blocks),
        out_specs=(in_hbm, in_hbm),
        scratch_shapes=[dma(2 * blocks)],
        compiler_params=pltpu.CompilerParams(vmem_limit_bytes=8 * 1024 * 1024),
    )(*done)


def solution(mesh):
    tensor = P("site", None, "sec", None, None)
    blocks = P("site", "sec", None, None)
    return jax.shard_map(
        per_device,
        mesh=mesh,
        in_specs=(tensor, tensor, tensor, blocks, blocks, blocks,
                  P("site", None, None), P("site", None), P("site")),
        out_specs=(tensor, tensor),
        check_vma=False,
    )
```

time: 49.7 us -> 44.1 us (0.89)
  Pallas kernels: 45.8 us -> 41.9 us
  local copies, waits for them, and re-layouts: 2.42 us -> 0.68 us
    pallas_call x1, Pallas kernels: 45.8 us -> 41 us  [per_device(): pl.pallas_call(functools.partial(kernel, steps, sites, parts, phys, owned...]
    unnamed x4, local copies, waits for them, and re-layouts: 2.42 us -> 0.68 us
    pallas_call x0 -> x1, Pallas kernels: none -> 0.93 us  [per_device(): pl.pallas_call(functools.partial(finish, phys, owned), out_shape=(shape,...]
where the time goes in v1:
time: 44.1 us; the launch traced here: 43.9 us
  Pallas kernels  41.9 us (95%)
  between operations  1.32 us (3%)
  local copies, waits for them, and re-layouts  0.68 us (2%)
    pallas_call x1, Pallas kernels, per_device(): pl.pallas_call(functools.partial(kernel, steps, sites, parts, phys, owned...  41 us
    pallas_call x1, Pallas kernels, per_device(): pl.pallas_call(functools.partial(finish, phys, owned), out_shape=(shape,...  0.93 us

profile of v1, /device:TPU:0, one launch (start us, length us, event | category | flops | bytes accessed | tf_op | source)
XLA Modules:
  0.0 43.9 jit_solution(13440118585044246594)
XLA Ops:
  0.6 0.0 copy-start.1
  1.3 0.0 copy-done.1
  1.3 0.0 copy-start
  1.3 0.7 %copy-done = s32[1,4,4]{2,1,0:T(4,128)S(1)} copy-done((s32[1,4,4]{2,1,0:T(4,128)S(1)}, s32[1,4,4]{2,1,0:T(4,128)}, u32[]{:S(2)}) %copy-start) | copy-done | bytes 88
  2.0 41.0 %shard_map.104 = (bf16[128,128]{1,0:T(8,128)(2,1)S(1)}, bf16[128,128]{1,0:T(8,128)(2,1)S(1)}, bf16[128,128]{1,0:T(8,128)(2,1)S(1)}, bf16[128,128]{1,0:T(8,128)(2...) custom-call(bf16[1,4,2,128,128]{4,3,2,1,0:T(8,128)(2,1)} %lc_in.1, ...), custom_call_target="tpu_custom_call" | custom-call | tf_op jit(solution)/shard_map/pallas_call | solution.py:427
  43.0 0.9 %shard_map.105 = (bf16[1,4,2,128,128]{4,3,2,1,0:T(8,128)(2,1)}, bf16[1,4,2,128,128]{4,3,2,1,0:T(8,128)(2,1)}) custom-call(bf16[128,128]{1,0:T(8,128)(2,1)S(1)} %get-tuple-element.18.refs_0_, bf16[128,128]{1,0:T(8,128)(2,1)S(1)} %get-tuple-element.19.refs_1_, bf16[128,128]{1,0:T(8,128)(2,1)S(1)} %get-tuple-element.20.refs_2_, ...), custom_call_target="tpu_custom_call" | custom-call | tf_op jit(solution)/shard_map/pallas_call | solution.py:467
Async XLA Ops:
  0.6 0.7 %copy-start.1 = (f32[1,4]{1,0:T(1,128)S(1)}, f32[1,4]{1,0:T(1,128)}, u32[]{:S(2)}) copy-start(f32[1,4]{1,0:T(1,128)} %onsite.1) | copy-start | bytes 52
  1.3 0.7 %copy-start = (s32[1,4,4]{2,1,0:T(4,128)S(1)}, s32[1,4,4]{2,1,0:T(4,128)}, u32[]{:S(2)}) copy-start(s32[1,4,4]{2,1,0:T(4,128)} %src.1) | copy-start | bytes 196

commit v2 on v1

--- a/solution.py
+++ b/solution.py
@@ -9,7 +9,6 @@
 
 NSI = 10
 NAPP = 2
-EARLY = 3
 VMEM_BYTES = 67043328
 RESERVED = 10240 * 1024
 SLACK = 44 * 1024
@@ -53,13 +52,13 @@
 
 def kernel(
     steps, sites, parts, phys, owned,
-    lc_in, rc_in, cs_in, cb_in, lseed_in, rseed_in, src, onsite, shift,
+    lc_in, rc_in, cs_in, cb_in, lseed_in, rseed_in, src_in, onsite_in, shift_in,
     *refs,
 ):
     blocks = phys * owned
     left_new, right_new = refs[:blocks], refs[blocks : 2 * blocks]
     (
-    lc, rc, cs, cb, lseed, rseed, site, fall,
+    lc, rc, cs, cb, lseed, rseed, src, onsite, shift, site, fall,
     hold_l, lrecv, lsend, rrecv, psend, terms, lct, bond, ys, zs, env_r,
     gsend, grecv, usend, urecv, tns, tnr, trs, trr,
     s_in, s_ls, s_lr, s_ps, s_pr, s_gs, s_gr, s_us, s_ur, s_tns, s_tnr, s_trs, s_trr,
@@ -78,6 +77,7 @@
     loads = [
         load(0, lseed_in, lseed), load(1, rseed_in, rseed), load(2, rc_in, rc),
         load(3, lc_in, lc), load(4, cb_in, cb), load(5, cs_in, cs),
+        load(6, src_in, src), load(7, onsite_in, onsite), load(8, shift_in, shift),
     ]
     for c in loads:
         c.start()
@@ -92,10 +92,12 @@
         )
 
     def c_seed(d):
-        return copy(lseed.at[0], lrecv.at[0, me], s_ls.at[steps, d], s_lr.at[0, me], j, sec(d))
-
-    def c_left(t, d):
-        return copy(lsend.at[t], lrecv.at[t + 1, me], s_ls.at[t, d], s_lr.at[t + 1, me], after, sec(d))
+        return copy(lseed.at[0], lrecv.at[0, me], s_ls.at[steps, d, 0], s_lr.at[0, me, 0], j, sec(d))
+
+    def c_left(t, d, k):
+        return copy(
+            lsend.at[t, k], lrecv.at[t + 1, me, k], s_ls.at[t, d, k], s_lr.at[t + 1, me, k], after, sec(d)
+        )
 
     def c_right(t, d):
         return copy(psend.at[t, d], rrecv.at[t, me], s_ps.at[t, d], s_pr.at[t, me], before, sec(d))
@@ -114,6 +116,10 @@
 
     def got(ref, sem):
         copy(ref, ref, s_us.at[0], sem, after, me).wait_recv()
+
+    def c_out(side, s, k):
+        a, b = (right_new, right_out) if side else (left_new, left_out)
+        return pltpu.make_async_copy(a.at[0, s, k], b.at[0, s, k], s_out.at[side, s, k])
 
     barrier = pltpu.get_barrier_semaphore()
     for d in range(parts):
@@ -126,6 +132,8 @@
     for d in range(1, parts):
         c_seed(d).start()
 
+    for c in loads[6:]:
+        c.wait()
     sources = [[src[0, s, off + k] for k in range(owned)] for s in range(phys)]
 
     def gathered(target):
@@ -160,15 +168,15 @@
             hold_l[off + k] = lseed[0, k]
         for d in range(1, parts):
             a = sec(d)
-            got(lrecv.at[0, a], s_lr.at[0, a])
+            got(lrecv.at[0, a], s_lr.at[0, a, 0])
             for k in range(owned):
                 hold_l[a * owned + k] = lrecv[0, a, k]
 
     def left_arrival(t):
         for d in range(parts):
             a = sec(d)
-            got(lrecv.at[t, a], s_lr.at[t, a])
             for k in range(owned):
+                got(lrecv.at[t, a, k], s_lr.at[t, a, k])
                 hold_l[a * owned + k] = lrecv[t, a, k]
 
     def right_arrival(t):
@@ -200,17 +208,18 @@
                 c_right(t, d).start()
 
     def left_compute(t, last):
+        prods = [
+            [dot(hold_l[sources[s][k]], lc[0, s, k]).astype(BF16) for s in range(phys)]
+            for k in range(owned)
+        ]
         for k in range(owned):
-            prods = [
-                dot(hold_l[sources[s][k]], lc[0, s, k]).astype(BF16) for s in range(phys)
-            ]
-            lsend[t, k] = dot(lct[k], jnp.concatenate(prods, axis=0)).astype(BF16)
-        if last:
-            tns[...] = traces([lsend[t, k] for k in range(owned)])
-            for d in range(1, parts):
-                c_tn(d).start()
-        for d in range(parts - 1, -1, -1):
-            c_left(t, d).start()
+            lsend[t, k] = dot(lct[k], below(prods[k])).astype(BF16)
+            if last and k == owned - 1:
+                tns[...] = traces([lsend[t, i] for i in range(owned)])
+                for d in range(1, parts):
+                    c_tn(d).start()
+            for d in range(parts - 1, -1, -1):
+                c_left(t, d, k).start()
 
     right_compute(0, steps == 1)
     loads[3].wait()
@@ -237,24 +246,27 @@
     def scale_of(total):
         return (sectors * width) / jnp.sum(total, axis=(0, 1), keepdims=True)
 
-    def begin(i, y, z, gram):
+    def begin(i, gram, block=None):
         norm = jnp.sqrt(jnp.sum(gram * gram, axis=(0, 1), keepdims=True))
-        root = lax.rsqrt(norm)
-        delta = (half_diagonal - 0.5 * (gram / norm)).astype(BF16)
-        if z is None:
-            y = gram / norm
-            zs[i] = diagonal + delta.astype(F32)
+        back, root = 1.0 / norm, 1.0 / jnp.sqrt(norm)
+        hi, lo = split(gram)
+        if block is None:
+            square = dot(beside((hi, lo)), twice_tall(hi))
+            first = gram * back
+            ys[i] = 1.5 * first - 0.5 * ((square * back) * back)
+            zs[i] = 1.5 * diagonal - 0.5 * first
         else:
-            y, z = y * root, z * root
-            zs[i] = z + dot(twice_wide(delta), below(split(z)))
-        ys[i] = y + dot(beside(split(y)), twice_tall(delta))
+            turned = block.T
+            ys[i] = (1.5 * block.astype(F32) - 0.5 * (dot(block, hi) * back)) * root
+            zs[i] = (1.5 * turned.astype(F32) - 0.5 * (dot(hi, turned) * back)) * root
         return root
 
-    def deltas(these):
+    def deltas(these, swap=False):
         zh = [split(zs[i]) for i in these]
         yh = [split(ys[i]) for i in these]
         found = [
-            (half_diagonal - 0.5 * dot(z[0], y[0])).astype(BF16) for z, y in zip(zh, yh)
+            (half_diagonal - 0.5 * (dot(y[0], z[0]) if swap else dot(z[0], y[0]))).astype(BF16)
+            for z, y in zip(zh, yh)
         ]
         return zh, yh, found
 
@@ -298,12 +310,11 @@
             half = dot(lsend[steps - 1, k], now[k]).astype(BF16)
             now[k] = (dot(half, env_r[k]) * scale + shift[0] * now[k].astype(F32)).astype(BF16)
     for k in range(owned):
-        begin(k, now[k].astype(F32), now[k].astype(F32).T, dot_tn(now[k], now[k]))
+        begin(bonds[k], dot_tn(now[k], now[k]), now[k])
     loads[5].wait()
     for k in range(owned):
         for s in range(phys):
             site[k, s * width : (s + 1) * width] = cs[0, s, k]
-    loop(EARLY, bonds)
 
     left_arrival(steps)
     scale = scale_of(traces([hold_l[m] for m in range(sectors)]))
@@ -330,14 +341,28 @@
             c_gram(d, p).start()
 
     left_root = [
-        begin(lefts[k], None, None, dot_tn(site[k], site[k])) for k in range(owned)
+        begin(lefts[k], dot_tn(site[k], site[k])) for k in range(owned)
     ]
-    loop(NSI - 1 - EARLY, bonds + lefts)
+    advance(bonds)
+    loop(NSI - 2, bonds + lefts)
     for k in range(owned):
         usend[k] = zs[k].astype(BF16)
     for d in range(parts - 1, -1, -1):
         c_unit(d).start()
-    loop(EARLY - 1, lefts)
+    packed = []
+    for p in range(pairs):
+        total, edge = gsend[p, :width], gsend[p, width:]
+        for d in range(1, parts):
+            a = sec(d)
+            got(grecv.at[a, p], s_gr.at[a, p])
+            total, edge = total + grecv[a, p, :width], edge + grecv[a, p, width:]
+        packed.append((total, jnp.sum(edge, axis=0, keepdims=True)))
+    right_root = []
+    for p, (total, line) in enumerate(packed):
+        turned = total.T
+        right_root.append(begin(rights[2 * p], jnp.where(rows >= cols, total, turned)))
+        odd = jnp.where(rows < cols, total, jnp.where(rows == cols, line, turned))
+        right_root.append(begin(rights[2 * p + 1], odd))
     zh, yh, found = deltas(lefts)
     for k in range(owned):
         hi, lo = split(zs[k])
@@ -348,20 +373,8 @@
         for s in range(phys):
             left_new[s * owned + k][...] = whole[s * width : (s + 1) * width]
 
-    right_root = []
-    for p in range(pairs):
-        total, edge = gsend[p, :width], gsend[p, width:]
-        for d in range(1, parts):
-            a = sec(d)
-            got(grecv.at[a, p], s_gr.at[a, p])
-            total, edge = total + grecv[a, p, :width], edge + grecv[a, p, width:]
-        turned = total.T
-        line = jnp.sum(edge, axis=0, keepdims=True)
-        right_root.append(begin(rights[2 * p], None, None, jnp.where(rows >= cols, total, turned)))
-        odd = jnp.where(rows < cols, total, jnp.where(rows == cols, line, turned))
-        right_root.append(begin(rights[2 * p + 1], None, None, odd))
     loop(NSI - 2, rights)
-    zh, yh, found = deltas(rights)
+    zh, yh, found = deltas(rights, swap=True)
     for a in range(parts):
         got(urecv.at[a], s_ur.at[a])
     for m in range(sectors):
@@ -376,7 +389,8 @@
 
     def drain(t, carry):
         for d in range(parts):
-            c_left(t, d).wait_send()
+            for k in range(owned):
+                c_left(t, d, k).wait_send()
             c_right(t, d).wait_send()
         return carry
 
@@ -420,18 +434,18 @@
 
     in_hbm = pl.BlockSpec(memory_space=pltpu.HBM)
     in_vmem = pl.BlockSpec(memory_space=pltpu.VMEM)
-    in_smem = pl.BlockSpec(memory_space=pltpu.SMEM)
     shape = jax.ShapeDtypeStruct(cs.shape, BF16)
     blocks = phys * owned
     room = VMEM_BYTES - RESERVED - 2 * cs.size * 2 - SLACK
     done = pl.pallas_call(
         functools.partial(kernel, steps, sites, parts, phys, owned),
         out_shape=[jax.ShapeDtypeStruct(block, BF16)] * (2 * blocks),
-        in_specs=[in_hbm] * 6 + [in_smem] * 3,
+        in_specs=[in_hbm] * 9,
         out_specs=[in_vmem] * (2 * blocks),
         scratch_shapes=[
             vm(*lc.shape), vm(*rc.shape), vm(*cs.shape), vm(*cb.shape),
             vm(*lseed.shape), vm(*rseed.shape),
+            pltpu.SMEM(src.shape, src.dtype), pltpu.SMEM(onsite.shape, F32), pltpu.SMEM(shift.shape, F32),
             vm(owned, phys * width, width), vm(sectors, *block),
             vm(sectors, *block),
             vm(steps + 1, parts, owned, *block),
@@ -452,8 +466,8 @@
             vm(parts, 8, width, dtype=F32),
             vm(8, width, dtype=F32),
             vm(parts, 8, width, dtype=F32),
-            dma(6),
-            dma(steps + 1, parts), dma(steps + 1, parts),
+            dma(9),
+            dma(steps + 1, parts, owned), dma(steps + 1, parts, owned),
             dma(steps, parts), dma(steps, parts),
             dma(parts, pairs), dma(parts, pairs),
             dma(parts), dma(parts),

time: 44.1 us -> 41.9 us (0.950)
  Pallas kernels: 41.9 us -> 39.7 us
    pallas_call x1, Pallas kernels: 41 us -> 38.8 us  [per_device(): pl.pallas_call(functools.partial(kernel, steps, sites, parts, phys, owned...]
where the time goes in v2:
time: 41.9 us; the launch traced here: 41.7 us
  Pallas kernels  39.7 us (95%)
  between operations  1.32 us (3%)
  local copies, waits for them, and re-layouts  0.68 us (2%)
    pallas_call x1, Pallas kernels, per_device(): pl.pallas_call(functools.partial(kernel, steps, sites, parts, phys, owned...  38.8 us
    pallas_call x1, Pallas kernels, per_device(): pl.pallas_call(functools.partial(finish, phys, owned), out_shape=(shape,...  0.93 us

profile of v2, /device:TPU:0, one launch (start us, length us, event | category | flops | bytes accessed | tf_op | source)
XLA Modules:
  0.0 41.7 jit_solution(3031617824986668054)
XLA Ops:
  0.6 0.0 copy-start.1
  1.3 0.0 copy-done.1
  1.3 0.0 copy-start
  1.3 0.7 %copy-done = s32[1,4,4]{2,1,0:T(4,128)S(1)} copy-done((s32[1,4,4]{2,1,0:T(4,128)S(1)}, s32[1,4,4]{2,1,0:T(4,128)}, u32[]{:S(2)}) %copy-start) | copy-done | bytes 88
  2.0 38.8 %shard_map.104 = (bf16[128,128]{1,0:T(8,128)(2,1)S(1)}, bf16[128,128]{1,0:T(8,128)(2,1)S(1)}, bf16[128,128]{1,0:T(8,128)(2,1)S(1)}, bf16[128,128]{1,0:T(8,128)(2...) custom-call(bf16[1,4,2,128,128]{4,3,2,1,0:T(8,128)(2,1)} %lc_in.1, ...), custom_call_target="tpu_custom_call" | custom-call | tf_op jit(solution)/shard_map/pallas_call | solution.py:440
  40.8 0.9 %shard_map.105 = (bf16[1,4,2,128,128]{4,3,2,1,0:T(8,128)(2,1)}, bf16[1,4,2,128,128]{4,3,2,1,0:T(8,128)(2,1)}) custom-call(bf16[128,128]{1,0:T(8,128)(2,1)S(1)} %get-tuple-element.18.refs_0_, bf16[128,128]{1,0:T(8,128)(2,1)S(1)} %get-tuple-element.19.refs_1_, bf16[128,128]{1,0:T(8,128)(2,1)S(1)} %get-tuple-element.20.refs_2_, ...), custom_call_target="tpu_custom_call" | custom-call | tf_op jit(solution)/shard_map/pallas_call | solution.py:481
Async XLA Ops:
  0.6 0.7 %copy-start.1 = (f32[1,4]{1,0:T(1,128)S(1)}, f32[1,4]{1,0:T(1,128)}, u32[]{:S(2)}) copy-start(f32[1,4]{1,0:T(1,128)} %onsite_in.1) | copy-start | bytes 52
  1.3 0.7 %copy-start = (s32[1,4,4]{2,1,0:T(4,128)S(1)}, s32[1,4,4]{2,1,0:T(4,128)}, u32[]{:S(2)}) copy-start(s32[1,4,4]{2,1,0:T(4,128)} %src_in.1) | copy-start | bytes 196

commit v3 on v2

--- a/solution.py
+++ b/solution.py
@@ -9,6 +9,7 @@
 
 NSI = 10
 NAPP = 2
+UNROLL = 4
 VMEM_BYTES = 67043328
 RESERVED = 10240 * 1024
 SLACK = 44 * 1024
@@ -278,10 +279,13 @@
 
     def loop(count, these):
         def body(n, carry):
+            for again in range(UNROLL):
+                advance(these)
+            return carry
+
+        lax.fori_loop(0, count // UNROLL, body, 0)
+        for again in range(count % UNROLL):
             advance(these)
-            return carry
-
-        lax.fori_loop(0, count, body, 0)
 
     bonds = list(range(owned))
     lefts = [owned + k for k in range(owned)]
@@ -297,20 +301,19 @@
     for k in range(owned):
         env_r[k] = (env_r[k].astype(F32) * scale).astype(BF16)
 
+    loads[4].wait()
+    now = [cb[0, k] for k in range(owned)]
+
+    def bond_product(k):
+        return dot(dot(lsend[steps - 1, k], now[k]).astype(BF16), env_r[k])
+
+    product = [bond_product(k) for k in range(owned)]
     total = tns[...]
     for d in range(1, parts):
         a = sec(d)
         got(tnr.at[a], s_tnr.at[a])
         total = total + tnr[a]
-    scale = scale_of(total)
-    loads[4].wait()
-    now = [cb[0, k] for k in range(owned)]
-    for repeat in range(NAPP):
-        for k in range(owned):
-            half = dot(lsend[steps - 1, k], now[k]).astype(BF16)
-            now[k] = (dot(half, env_r[k]) * scale + shift[0] * now[k].astype(F32)).astype(BF16)
-    for k in range(owned):
-        begin(bonds[k], dot_tn(now[k], now[k]), now[k])
+    bond_scale = scale_of(total)
     loads[5].wait()
     for k in range(owned):
         for s in range(phys):
@@ -340,15 +343,32 @@
         for d in range(1, parts):
             c_gram(d, p).start()
 
+    for repeat in range(NAPP):
+        if repeat > 0:
+            product = [bond_product(k) for k in range(owned)]
+        for k in range(owned):
+            now[k] = (product[k] * bond_scale + shift[0] * now[k].astype(F32)).astype(BF16)
+    for k in range(owned):
+        begin(bonds[k], dot_tn(now[k], now[k]), now[k])
     left_root = [
         begin(lefts[k], dot_tn(site[k], site[k])) for k in range(owned)
     ]
+    loop(NSI - 2, bonds + lefts)
     advance(bonds)
-    loop(NSI - 2, bonds + lefts)
     for k in range(owned):
         usend[k] = zs[k].astype(BF16)
     for d in range(parts - 1, -1, -1):
         c_unit(d).start()
+    zh, yh, found = deltas(lefts)
+    for k in range(owned):
+        hi, lo = split(zs[k])
+        wide = dot(beside(zh[k]), beside((twice_tall(hi), twice_tall(lo))))
+        value = wide[:, :width] + wide[:, width:]
+        factor = value + dot(twice_wide(found[k]), below(split(value)))
+        whole = dot(site[k], (factor * left_root[k]).astype(BF16)).astype(BF16)
+        for s in range(phys):
+            left_new[s * owned + k][...] = whole[s * width : (s + 1) * width]
+
     packed = []
     for p in range(pairs):
         total, edge = gsend[p, :width], gsend[p, width:]
@@ -363,24 +383,15 @@
         right_root.append(begin(rights[2 * p], jnp.where(rows >= cols, total, turned)))
         odd = jnp.where(rows < cols, total, jnp.where(rows == cols, line, turned))
         right_root.append(begin(rights[2 * p + 1], odd))
-    zh, yh, found = deltas(lefts)
-    for k in range(owned):
-        hi, lo = split(zs[k])
-        wide = dot(beside(zh[k]), beside((twice_tall(hi), twice_tall(lo))))
-        value = wide[:, :width] + wide[:, width:]
-        factor = value + dot(twice_wide(found[k]), below(split(value)))
-        whole = dot(site[k], (factor * left_root[k]).astype(BF16)).astype(BF16)
-        for s in range(phys):
-            left_new[s * owned + k][...] = whole[s * width : (s + 1) * width]
-
     loop(NSI - 2, rights)
-    zh, yh, found = deltas(rights, swap=True)
     for a in range(parts):
         got(urecv.at[a], s_ur.at[a])
+    zh, yh, found = deltas(rights, swap=True)
+    values = [
+        dot(twice_wide(urecv[m // owned, m % owned]), below(zh[m])) for m in range(sectors)
+    ]
     for m in range(sectors):
-        unit = urecv[m // owned, m % owned]
-        value = dot(twice_wide(unit), below(zh[m]))
-        factor = value + dot(beside(split(value)), twice_tall(found[m]))
+        factor = values[m] + dot(beside(split(values[m])), twice_tall(found[m]))
         fall[m] = (factor * right_root[m]).astype(BF16)
     for k in range(owned):
         for s in range(phys):

time: 41.9 us -> 40.2 us (0.959)
  Pallas kernels: 39.7 us -> 38 us
    pallas_call x1, Pallas kernels: 38.8 us -> 37.1 us  [per_device(): pl.pallas_call(functools.partial(kernel, steps, sites, parts, phys, owned...]
where the time goes in v3:
time: 40.2 us; the launch traced here: 40 us
  Pallas kernels  38 us (95%)
  between operations  1.32 us (3%)
  local copies, waits for them, and re-layouts  0.68 us (2%)
    pallas_call x1, Pallas kernels, per_device(): pl.pallas_call(functools.partial(kernel, steps, sites, parts, phys, owned...  37.1 us
    pallas_call x1, Pallas kernels, per_device(): pl.pallas_call(functools.partial(finish, phys, owned), out_shape=(shape,...  0.93 us

profile of v3, /device:TPU:0, one launch (start us, length us, event | category | flops | bytes accessed | tf_op | source)
XLA Modules:
  0.0 40.0 jit_solution(12952453437749892205)
XLA Ops:
  0.6 0.0 copy-start.1
  1.3 0.0 copy-done.1
  1.3 0.0 copy-start
  1.3 0.7 %copy-done = s32[1,4,4]{2,1,0:T(4,128)S(1)} copy-done((s32[1,4,4]{2,1,0:T(4,128)S(1)}, s32[1,4,4]{2,1,0:T(4,128)}, u32[]{:S(2)}) %copy-start) | copy-done | bytes 88
  2.0 37.1 %shard_map.104 = (bf16[128,128]{1,0:T(8,128)(2,1)S(1)}, bf16[128,128]{1,0:T(8,128)(2,1)S(1)}, bf16[128,128]{1,0:T(8,128)(2,1)S(1)}, bf16[128,128]{1,0:T(8,128)(2...) custom-call(bf16[1,4,2,128,128]{4,3,2,1,0:T(8,128)(2,1)} %lc_in.1, ...), custom_call_target="tpu_custom_call" | custom-call | tf_op jit(solution)/shard_map/pallas_call | solution.py:451
  39.1 0.9 %shard_map.105 = (bf16[1,4,2,128,128]{4,3,2,1,0:T(8,128)(2,1)}, bf16[1,4,2,128,128]{4,3,2,1,0:T(8,128)(2,1)}) custom-call(bf16[128,128]{1,0:T(8,128)(2,1)S(1)} %get-tuple-element.18.refs_0_, bf16[128,128]{1,0:T(8,128)(2,1)S(1)} %get-tuple-element.19.refs_1_, bf16[128,128]{1,0:T(8,128)(2,1)S(1)} %get-tuple-element.20.refs_2_, ...), custom_call_target="tpu_custom_call" | custom-call | tf_op jit(solution)/shard_map/pallas_call | solution.py:492
Async XLA Ops:
  0.6 0.7 %copy-start.1 = (f32[1,4]{1,0:T(1,128)S(1)}, f32[1,4]{1,0:T(1,128)}, u32[]{:S(2)}) copy-start(f32[1,4]{1,0:T(1,128)} %onsite_in.1) | copy-start | bytes 52
  1.3 0.7 %copy-start = (s32[1,4,4]{2,1,0:T(4,128)S(1)}, s32[1,4,4]{2,1,0:T(4,128)}, u32[]{:S(2)}) copy-start(s32[1,4,4]{2,1,0:T(4,128)} %src_in.1) | copy-start | bytes 196

commit v4 on v3

--- a/solution.py
+++ b/solution.py
@@ -9,7 +9,7 @@
 
 NSI = 10
 NAPP = 2
-UNROLL = 4
+UNROLL = 8
 VMEM_BYTES = 67043328
 RESERVED = 10240 * 1024
 SLACK = 44 * 1024
@@ -219,8 +219,10 @@
                 tns[...] = traces([lsend[t, i] for i in range(owned)])
                 for d in range(1, parts):
                     c_tn(d).start()
-            for d in range(parts - 1, -1, -1):
+            for d in range(parts - 1, 0, -1):
                 c_left(t, d, k).start()
+        for k in range(owned):
+            c_left(t, 0, k).start()
 
     right_compute(0, steps == 1)
     loads[3].wait()
@@ -308,41 +310,41 @@
         return dot(dot(lsend[steps - 1, k], now[k]).astype(BF16), env_r[k])
 
     product = [bond_product(k) for k in range(owned)]
+    loads[5].wait()
+
+    left_arrival(steps)
+    scale = scale_of(traces([hold_l[m] for m in range(sectors)]))
+    states = [[cs[0, s, k] for s in range(phys)] for k in range(owned)]
+    for repeat in range(NAPP):
+        halves = [
+            [dot(hold_l[sources[s][k]], states[k][s]).astype(BF16) for s in range(phys)]
+            for k in range(owned)
+        ]
+        for k in range(owned):
+            whole = dot(below(halves[k]), env_r[k]) * scale
+            states[k] = [
+                (whole[s * width : (s + 1) * width] + onsite[0, s] * states[k][s].astype(F32)).astype(BF16)
+                for s in range(phys)
+            ]
+    for k in range(owned):
+        site[k] = below(states[k])
+
+    for k in range(owned):
+        for s in range(phys):
+            terms[s * owned + k] = dot_nt(states[k][s], states[k][s])
+    for p in range(pairs):
+        even, odd = gathered(2 * p), gathered(2 * p + 1)
+        gsend[p, :width] = jnp.where(rows >= cols, even, odd)
+        gsend[p, width:] = jnp.sum((odd * diagonal).reshape(width // 8, 8, width), axis=0)
+        for d in range(1, parts):
+            c_gram(d, p).start()
+
     total = tns[...]
     for d in range(1, parts):
         a = sec(d)
         got(tnr.at[a], s_tnr.at[a])
         total = total + tnr[a]
     bond_scale = scale_of(total)
-    loads[5].wait()
-    for k in range(owned):
-        for s in range(phys):
-            site[k, s * width : (s + 1) * width] = cs[0, s, k]
-
-    left_arrival(steps)
-    scale = scale_of(traces([hold_l[m] for m in range(sectors)]))
-    for repeat in range(NAPP):
-        for k in range(owned):
-            halves = [
-                dot(hold_l[sources[s][k]], site[k, s * width : (s + 1) * width]).astype(BF16)
-                for s in range(phys)
-            ]
-            whole = dot(jnp.concatenate(halves, axis=0), env_r[k]) * scale
-            for s in range(phys):
-                part = slice(s * width, (s + 1) * width)
-                site[k, part] = (whole[part] + onsite[0, s] * site[k, part].astype(F32)).astype(BF16)
-
-    for k in range(owned):
-        for s in range(phys):
-            block = site[k, s * width : (s + 1) * width]
-            terms[s * owned + k] = dot_nt(block, block)
-    for p in range(pairs):
-        even, odd = gathered(2 * p), gathered(2 * p + 1)
-        gsend[p, :width] = jnp.where(rows >= cols, even, odd)
-        gsend[p, width:] = jnp.sum((odd * diagonal).reshape(width // 8, 8, width), axis=0)
-        for d in range(1, parts):
-            c_gram(d, p).start()
-
     for repeat in range(NAPP):
         if repeat > 0:
             product = [bond_product(k) for k in range(owned)]

time: 40.2 us -> 39.7 us (0.988)
  Pallas kernels: 38 us -> 37.5 us
    pallas_call x1, Pallas kernels: 37.1 us -> 36.6 us  [per_device(): pl.pallas_call(functools.partial(kernel, steps, sites, parts, phys, owned...]
where the time goes in v4:
time: 39.7 us; the launch traced here: 39.5 us
  Pallas kernels  37.5 us (94%)
  between operations  1.32 us (3%)
  local copies, waits for them, and re-layouts  0.68 us (2%)
    pallas_call x1, Pallas kernels, per_device(): pl.pallas_call(functools.partial(kernel, steps, sites, parts, phys, owned...  36.6 us
    pallas_call x1, Pallas kernels, per_device(): pl.pallas_call(functools.partial(finish, phys, owned), out_shape=(shape,...  0.93 us

profile of v4, /device:TPU:0, one launch (start us, length us, event | category | flops | bytes accessed | tf_op | source)
XLA Modules:
  0.0 39.5 jit_solution(9636553427937847038)
XLA Ops:
  0.6 0.0 copy-start.1
  1.3 0.0 copy-done.1
  1.3 0.0 copy-start
  1.3 0.7 %copy-done = s32[1,4,4]{2,1,0:T(4,128)S(1)} copy-done((s32[1,4,4]{2,1,0:T(4,128)S(1)}, s32[1,4,4]{2,1,0:T(4,128)}, u32[]{:S(2)}) %copy-start) | copy-done | bytes 88
  2.0 36.6 %shard_map.104 = (bf16[128,128]{1,0:T(8,128)(2,1)S(1)}, bf16[128,128]{1,0:T(8,128)(2,1)S(1)}, bf16[128,128]{1,0:T(8,128)(2,1)S(1)}, bf16[128,128]{1,0:T(8,128)(2...) custom-call(bf16[1,4,2,128,128]{4,3,2,1,0:T(8,128)(2,1)} %lc_in.1, ...), custom_call_target="tpu_custom_call" | custom-call | tf_op jit(solution)/shard_map/pallas_call | solution.py:453
  38.6 0.9 %shard_map.105 = (bf16[1,4,2,128,128]{4,3,2,1,0:T(8,128)(2,1)}, bf16[1,4,2,128,128]{4,3,2,1,0:T(8,128)(2,1)}) custom-call(bf16[128,128]{1,0:T(8,128)(2,1)S(1)} %get-tuple-element.18.refs_0_, bf16[128,128]{1,0:T(8,128)(2,1)S(1)} %get-tuple-element.19.refs_1_, bf16[128,128]{1,0:T(8,128)(2,1)S(1)} %get-tuple-element.20.refs_2_, ...), custom_call_target="tpu_custom_call" | custom-call | tf_op jit(solution)/shard_map/pallas_call | solution.py:494
Async XLA Ops:
  0.6 0.7 %copy-start.1 = (f32[1,4]{1,0:T(1,128)S(1)}, f32[1,4]{1,0:T(1,128)}, u32[]{:S(2)}) copy-start(f32[1,4]{1,0:T(1,128)} %onsite_in.1) | copy-start | bytes 52
  1.3 0.7 %copy-start = (s32[1,4,4]{2,1,0:T(4,128)S(1)}, s32[1,4,4]{2,1,0:T(4,128)}, u32[]{:S(2)}) copy-start(s32[1,4,4]{2,1,0:T(4,128)} %src_in.1) | copy-start | bytes 196

commit v5 on v4

--- a/solution.py
+++ b/solution.py
@@ -56,14 +56,14 @@
     lc_in, rc_in, cs_in, cb_in, lseed_in, rseed_in, src_in, onsite_in, shift_in,
     *refs,
 ):
-    blocks = phys * owned
-    left_new, right_new = refs[:blocks], refs[blocks : 2 * blocks]
+    left_new, right_new = refs[:phys], refs[phys : 2 * phys]
+    lrecv = refs[2 * phys : 2 * phys + steps + 1]
     (
     lc, rc, cs, cb, lseed, rseed, src, onsite, shift, site, fall,
-    hold_l, lrecv, lsend, rrecv, psend, terms, lct, bond, ys, zs, env_r,
+    lsend, rrecv, psend, terms, lct, bond, ys, zs, env_r,
     gsend, grecv, usend, urecv, tns, tnr, trs, trr,
     s_in, s_ls, s_lr, s_ps, s_pr, s_gs, s_gr, s_us, s_ur, s_tns, s_tnr, s_trs, s_trr,
-    ) = refs[2 * blocks :]
+    ) = refs[2 * phys + steps + 1 :]
     j = lax.axis_index("site")
     me = lax.axis_index("sec")
     after, before = lax.rem(j + 1, sites), lax.rem(j + sites - 1, sites)
@@ -93,11 +93,11 @@
         )
 
     def c_seed(d):
-        return copy(lseed.at[0], lrecv.at[0, me], s_ls.at[steps, d, 0], s_lr.at[0, me, 0], j, sec(d))
+        return copy(lseed.at[0], lrecv[0].at[pl.ds(off, owned)], s_ls.at[steps, d, 0], s_lr.at[0, me, 0], j, sec(d))
 
     def c_left(t, d, k):
         return copy(
-            lsend.at[t, k], lrecv.at[t + 1, me, k], s_ls.at[t, d, k], s_lr.at[t + 1, me, k], after, sec(d)
+            lsend.at[t, k], lrecv[t + 1].at[off + k], s_ls.at[t, d, k], s_lr.at[t + 1, me, k], after, sec(d)
         )
 
     def c_right(t, d):
@@ -166,19 +166,16 @@
 
     def seed_arrival():
         for k in range(owned):
-            hold_l[off + k] = lseed[0, k]
+            lrecv[0][off + k] = lseed[0, k]
         for d in range(1, parts):
             a = sec(d)
-            got(lrecv.at[0, a], s_lr.at[0, a, 0])
-            for k in range(owned):
-                hold_l[a * owned + k] = lrecv[0, a, k]
+            got(lrecv[0].at[pl.ds(a * owned, owned)], s_lr.at[0, a, 0])
 
     def left_arrival(t):
         for d in range(parts):
             a = sec(d)
             for k in range(owned):
-                got(lrecv.at[t, a, k], s_lr.at[t, a, k])
-                hold_l[a * owned + k] = lrecv[t, a, k]
+                got(lrecv[t].at[a * owned + k], s_lr.at[t, a, k])
 
     def right_arrival(t):
         for d in range(parts):
@@ -210,7 +207,7 @@
 
     def left_compute(t, last):
         prods = [
-            [dot(hold_l[sources[s][k]], lc[0, s, k]).astype(BF16) for s in range(phys)]
+            [dot(lrecv[t][sources[s][k]], lc[0, s, k]).astype(BF16) for s in range(phys)]
             for k in range(owned)
         ]
         for k in range(owned):
@@ -232,19 +229,11 @@
     seed_arrival()
     left_compute(0, steps == 1)
 
-    def turn(t, carry):
+    for t in range(1, steps):
         right_arrival(t - 1)
-        right_compute(t, False)
+        right_compute(t, t == steps - 1)
         left_arrival(t)
-        left_compute(t, False)
-        return carry
-
-    lax.fori_loop(1, steps - 1, turn, 0)
-    if steps > 1:
-        right_arrival(steps - 2)
-        right_compute(steps - 1, True)
-        left_arrival(steps - 1)
-        left_compute(steps - 1, True)
+        left_compute(t, t == steps - 1)
 
     def scale_of(total):
         return (sectors * width) / jnp.sum(total, axis=(0, 1), keepdims=True)
@@ -313,11 +302,11 @@
     loads[5].wait()
 
     left_arrival(steps)
-    scale = scale_of(traces([hold_l[m] for m in range(sectors)]))
+    scale = scale_of(traces([lrecv[steps][m] for m in range(sectors)]))
     states = [[cs[0, s, k] for s in range(phys)] for k in range(owned)]
     for repeat in range(NAPP):
         halves = [
-            [dot(hold_l[sources[s][k]], states[k][s]).astype(BF16) for s in range(phys)]
+            [dot(lrecv[steps][sources[s][k]], states[k][s]).astype(BF16) for s in range(phys)]
             for k in range(owned)
         ]
         for k in range(owned):
@@ -355,8 +344,8 @@
     left_root = [
         begin(lefts[k], dot_tn(site[k], site[k])) for k in range(owned)
     ]
+    advance(bonds)
     loop(NSI - 2, bonds + lefts)
-    advance(bonds)
     for k in range(owned):
         usend[k] = zs[k].astype(BF16)
     for d in range(parts - 1, -1, -1):
@@ -369,8 +358,18 @@
         factor = value + dot(twice_wide(found[k]), below(split(value)))
         whole = dot(site[k], (factor * left_root[k]).astype(BF16)).astype(BF16)
         for s in range(phys):
-            left_new[s * owned + k][...] = whole[s * width : (s + 1) * width]
-
+            left_new[s][k] = whole[s * width : (s + 1) * width]
+
+    for t in range(steps):
+        for d in range(parts):
+            for k in range(owned):
+                c_left(t, d, k).wait_send()
+            c_right(t, d).wait_send()
+    for d in range(parts):
+        c_tr(d).wait_send()
+    for d in range(1, parts):
+        c_seed(d).wait_send()
+        c_tn(d).wait_send()
     packed = []
     for p in range(pairs):
         total, edge = gsend[p, :width], gsend[p, width:]
@@ -398,34 +397,21 @@
     for k in range(owned):
         for s in range(phys):
             block = site[k, s * width : (s + 1) * width]
-            right_new[s * owned + k][...] = dot(fall[sources[s][k]], block).astype(BF16)
-
-    def drain(t, carry):
-        for d in range(parts):
-            for k in range(owned):
-                c_left(t, d, k).wait_send()
-            c_right(t, d).wait_send()
-        return carry
-
-    lax.fori_loop(0, steps, drain, 0)
+            right_new[s][k] = dot(fall[sources[s][k]], block).astype(BF16)
+
     for d in range(parts):
-        c_tr(d).wait_send()
         c_unit(d).wait_send()
     for d in range(1, parts):
-        c_seed(d).wait_send()
-        c_tn(d).wait_send()
         for p in range(pairs):
             c_gram(d, p).wait_send()
 
 
-def finish(phys, owned, *refs):
-    blocks = phys * owned
-    left_new, right_new, sems = refs[2 * blocks :]
+def finish(phys, *refs):
+    left_new, right_new, sems = refs[2 * phys :]
     copies = []
-    for i in range(2 * blocks):
-        out = left_new if i < blocks else right_new
-        s, k = (i % blocks) // owned, i % owned
-        copies.append(pltpu.make_async_copy(refs[i], out.at[0, s, k], sems.at[i]))
+    for i in range(2 * phys):
+        out = left_new if i < phys else right_new
+        copies.append(pltpu.make_async_copy(refs[i], out.at[0, i % phys], sems.at[i]))
         copies[-1].start()
     for c in copies:
         c.wait()
@@ -448,20 +434,17 @@
     in_hbm = pl.BlockSpec(memory_space=pltpu.HBM)
     in_vmem = pl.BlockSpec(memory_space=pltpu.VMEM)
     shape = jax.ShapeDtypeStruct(cs.shape, BF16)
-    blocks = phys * owned
     room = VMEM_BYTES - RESERVED - 2 * cs.size * 2 - SLACK
     done = pl.pallas_call(
         functools.partial(kernel, steps, sites, parts, phys, owned),
-        out_shape=[jax.ShapeDtypeStruct(block, BF16)] * (2 * blocks),
+        out_shape=[jax.ShapeDtypeStruct((owned, *block), BF16)] * (2 * phys),
         in_specs=[in_hbm] * 9,
-        out_specs=[in_vmem] * (2 * blocks),
-        scratch_shapes=[
+        out_specs=[in_vmem] * (2 * phys),
+        scratch_shapes=[vm(sectors, *block)] * (steps + 1) + [
             vm(*lc.shape), vm(*rc.shape), vm(*cs.shape), vm(*cb.shape),
             vm(*lseed.shape), vm(*rseed.shape),
             pltpu.SMEM(src.shape, src.dtype), pltpu.SMEM(onsite.shape, F32), pltpu.SMEM(shift.shape, F32),
             vm(owned, phys * width, width), vm(sectors, *block),
-            vm(sectors, *block),
-            vm(steps + 1, parts, owned, *block),
             vm(steps, owned, *block),
             vm(steps, parts, owned, *block),
             vm(steps, parts, owned, *block),
@@ -492,11 +475,11 @@
         ),
     )(lc, rc, cs, cb, lseed, rseed, src, onsite, shift)
     return pl.pallas_call(
-        functools.partial(finish, phys, owned),
+        functools.partial(finish, phys),
         out_shape=(shape, shape),
-        in_specs=[in_vmem] * (2 * blocks),
+        in_specs=[in_vmem] * (2 * phys),
         out_specs=(in_hbm, in_hbm),
-        scratch_shapes=[dma(2 * blocks)],
+        scratch_shapes=[dma(2 * phys)],
         compiler_params=pltpu.CompilerParams(vmem_limit_bytes=8 * 1024 * 1024),
     )(*done)
 

time: 39.7 us -> 39.6 us (level)
  no operation moved by 1% of the time
where the time goes in v5:
time: 39.6 us; the launch traced here: 39.4 us
  Pallas kernels  37.4 us (94%)
  between operations  1.32 us (3%)
  local copies, waits for them, and re-layouts  0.68 us (2%)
    pallas_call x1, Pallas kernels, per_device(): pl.pallas_call(functools.partial(kernel, steps, sites, parts, phys, owned...  36.5 us
    pallas_call x1, Pallas kernels, per_device(): pl.pallas_call(functools.partial(finish, phys), out_shape=(shape, shape),...  0.85 us

profile of v5, /device:TPU:0, one launch (start us, length us, event | category | flops | bytes accessed | tf_op | source)
XLA Modules:
  0.0 39.4 jit_solution(14112958195515277314)
XLA Ops:
  0.6 0.0 copy-start.1
  1.3 0.0 copy-done.1
  1.3 0.0 copy-start
  1.3 0.7 %copy-done = s32[1,4,4]{2,1,0:T(4,128)S(1)} copy-done((s32[1,4,4]{2,1,0:T(4,128)S(1)}, s32[1,4,4]{2,1,0:T(4,128)}, u32[]{:S(2)}) %copy-start) | copy-done | bytes 88
  2.0 36.5 %shard_map.104 = (bf16[2,128,128]{2,1,0:T(8,128)(2,1)S(1)}, bf16[2,128,128]{2,1,0:T(8,128)(2,1)S(1)}, bf16[2,128,128]{2,1,0:T(8,128)(2,1)S(1)}, bf16[2,128,128]{...) custom-call(bf16[1,4,2,128,128]{4,3,2,1,0:T(8,128)(2,1)} %lc_in.1, ...), custom_call_target="tpu_custom_call" | custom-call | tf_op jit(solution)/shard_map/pallas_call | solution.py:438
  38.5 0.9 %shard_map.105 = (bf16[1,4,2,128,128]{4,3,2,1,0:T(8,128)(2,1)}, bf16[1,4,2,128,128]{4,3,2,1,0:T(8,128)(2,1)}) custom-call(bf16[2,128,128]{2,1,0:T(8,128)(2,1)S(1)} %get-tuple-element.10.refs_0_, bf16[2,128,128]{2,1,0:T(8,128)(2,1)S(1)} %get-tuple-element.11.refs_1_, bf16[2,128,128]{2,1,0:T(8,128)(2,1)S(1)} %get-tuple-element.12.refs_2_, ...), custom_call_target="tpu_custom_call" | custom-call | tf_op jit(solution)/shard_map/pallas_call | solution.py:477
Async XLA Ops:
  0.6 0.7 %copy-start.1 = (f32[1,4]{1,0:T(1,128)S(1)}, f32[1,4]{1,0:T(1,128)}, u32[]{:S(2)}) copy-start(f32[1,4]{1,0:T(1,128)} %onsite_in.1) | copy-start | bytes 52
  1.3 0.7 %copy-start = (s32[1,4,4]{2,1,0:T(4,128)S(1)}, s32[1,4,4]{2,1,0:T(4,128)}, u32[]{:S(2)}) copy-start(s32[1,4,4]{2,1,0:T(4,128)} %src_in.1) | copy-start | bytes 196

commit v6 on v5

--- a/solution.py
+++ b/solution.py
@@ -60,7 +60,7 @@
     lrecv = refs[2 * phys : 2 * phys + steps + 1]
     (
     lc, rc, cs, cb, lseed, rseed, src, onsite, shift, site, fall,
-    lsend, rrecv, psend, terms, lct, bond, ys, zs, env_r,
+    ahead, lsend, rrecv, psend, terms, lct, bond, ys, zs, env_r,
     gsend, grecv, usend, urecv, tns, tnr, trs, trr,
     s_in, s_ls, s_lr, s_ps, s_pr, s_gs, s_gr, s_us, s_ur, s_tns, s_tnr, s_trs, s_trr,
     ) = refs[2 * phys + steps + 1 :]
@@ -300,21 +300,37 @@
 
     product = [bond_product(k) for k in range(owned)]
     loads[5].wait()
+    for k in range(owned):
+        ahead[k] = dot(below([cs[0, s, k] for s in range(phys)]), env_r[k]).astype(BF16)
 
     left_arrival(steps)
     scale = scale_of(traces([lrecv[steps][m] for m in range(sectors)]))
     states = [[cs[0, s, k] for s in range(phys)] for k in range(owned)]
     for repeat in range(NAPP):
-        halves = [
-            [dot(lrecv[steps][sources[s][k]], states[k][s]).astype(BF16) for s in range(phys)]
+        if repeat == 0:
+            wholes = [
+                [
+                    dot(lrecv[steps][sources[s][k]], ahead[k, s * width : (s + 1) * width])
+                    for s in range(phys)
+                ]
+                for k in range(owned)
+            ]
+        else:
+            halves = [
+                [dot(lrecv[steps][sources[s][k]], states[k][s]).astype(BF16) for s in range(phys)]
+                for k in range(owned)
+            ]
+            wholes = [dot(below(halves[k]), env_r[k]) for k in range(owned)]
+            wholes = [
+                [whole[s * width : (s + 1) * width] for s in range(phys)] for whole in wholes
+            ]
+        states = [
+            [
+                (wholes[k][s] * scale + onsite[0, s] * states[k][s].astype(F32)).astype(BF16)
+                for s in range(phys)
+            ]
             for k in range(owned)
         ]
-        for k in range(owned):
-            whole = dot(below(halves[k]), env_r[k]) * scale
-            states[k] = [
-                (whole[s * width : (s + 1) * width] + onsite[0, s] * states[k][s].astype(F32)).astype(BF16)
-                for s in range(phys)
-            ]
     for k in range(owned):
         site[k] = below(states[k])
 
@@ -445,6 +461,7 @@
             vm(*lseed.shape), vm(*rseed.shape),
             pltpu.SMEM(src.shape, src.dtype), pltpu.SMEM(onsite.shape, F32), pltpu.SMEM(shift.shape, F32),
             vm(owned, phys * width, width), vm(sectors, *block),
+            vm(owned, phys * width, width),
             vm(steps, owned, *block),
             vm(steps, parts, owned, *block),
             vm(steps, parts, owned, *block),

time: 39.6 us -> 39.5 us (level)
  no operation moved by 1% of the time
where the time goes in v6:
time: 39.5 us; the launch traced here: 39.3 us
  Pallas kernels  37.3 us (94%)
  between operations  1.32 us (3%)
  local copies, waits for them, and re-layouts  0.68 us (2%)
    pallas_call x1, Pallas kernels, per_device(): pl.pallas_call(functools.partial(kernel, steps, sites, parts, phys, owned...  36.5 us
    pallas_call x1, Pallas kernels, per_device(): pl.pallas_call(functools.partial(finish, phys), out_shape=(shape, shape),...  0.85 us

profile of v6, /device:TPU:0, one launch (start us, length us, event | category | flops | bytes accessed | tf_op | source)
XLA Modules:
  0.0 39.3 jit_solution(16267052101807179596)
XLA Ops:
  0.6 0.0 copy-start.1
  1.3 0.0 copy-done.1
  1.3 0.0 copy-start
  1.3 0.7 %copy-done = s32[1,4,4]{2,1,0:T(4,128)S(1)} copy-done((s32[1,4,4]{2,1,0:T(4,128)S(1)}, s32[1,4,4]{2,1,0:T(4,128)}, u32[]{:S(2)}) %copy-start) | copy-done | bytes 88
  2.0 36.5 %shard_map.104 = (bf16[2,128,128]{2,1,0:T(8,128)(2,1)S(1)}, bf16[2,128,128]{2,1,0:T(8,128)(2,1)S(1)}, bf16[2,128,128]{2,1,0:T(8,128)(2,1)S(1)}, bf16[2,128,128]{...) custom-call(bf16[1,4,2,128,128]{4,3,2,1,0:T(8,128)(2,1)} %lc_in.1, ...), custom_call_target="tpu_custom_call" | custom-call | tf_op jit(solution)/shard_map/pallas_call | solution.py:454
  38.5 0.9 %shard_map.105 = (bf16[1,4,2,128,128]{4,3,2,1,0:T(8,128)(2,1)}, bf16[1,4,2,128,128]{4,3,2,1,0:T(8,128)(2,1)}) custom-call(bf16[2,128,128]{2,1,0:T(8,128)(2,1)S(1)} %get-tuple-element.10.refs_0_, bf16[2,128,128]{2,1,0:T(8,128)(2,1)S(1)} %get-tuple-element.11.refs_1_, bf16[2,128,128]{2,1,0:T(8,128)(2,1)S(1)} %get-tuple-element.12.refs_2_, ...), custom_call_target="tpu_custom_call" | custom-call | tf_op jit(solution)/shard_map/pallas_call | solution.py:494
Async XLA Ops:
  0.6 0.7 %copy-start.1 = (f32[1,4]{1,0:T(1,128)S(1)}, f32[1,4]{1,0:T(1,128)}, u32[]{:S(2)}) copy-start(f32[1,4]{1,0:T(1,128)} %onsite_in.1) | copy-start | bytes 52
  1.3 0.7 %copy-start = (s32[1,4,4]{2,1,0:T(4,128)S(1)}, s32[1,4,4]{2,1,0:T(4,128)}, u32[]{:S(2)}) copy-start(s32[1,4,4]{2,1,0:T(4,128)} %src_in.1) | copy-start | bytes 196
